TPU v7x, 32 devices: a whole 2x2x4 slice. The times are simulated.
32 devices in a mesh: rep: 16 (over z, y, x), shard: 2 (over core).
Axes of the slice: x: 2, y: 2, z: 4, core: 2. Of those that a mesh axis runs over, the one named last changes fastest.
Arguments:
- outer_params: float32 [4, 131072], P('shard'), may hold values from -6 to 6
- replica_delta: float32 [16, 4, 131072], P('rep', 'shard'), may hold values from -20 to 20
- momentum: float32 [4, 131072], P('shard', 'rep'), may hold values from -20 to 20
- tensor_of_block: int32 [4], P('shard'), may hold values from 0 to 1, as said below
Outputs:
- new_params: float32 [4, 131072], P('shard')
- new_momentum: float32 [4, 131072], P('shard', 'rep')
Inputs may be any that keep to these rules, and one draw needn't show every extreme that they name: `tensor_of_block`: every tensor owns exactly 2 blocks.
All inputs are finite; a program needn't handle non-finite values.
Results may differ from a plain program's by a relative error of at most 0.00028.
Values sent between devices are 32-bit elements; how exact they have to be, the bound alone decides.
A program may use at most 64 MiB of HBM per device.

v0:
```python
import functools

import jax
import jax.numpy as jnp
from jax import lax
from jax.experimental import pallas as pl
from jax.experimental.pallas import tpu as pltpu
from jax.sharding import PartitionSpec as P

BLOCK_ROWS = 128
BLOCK_COLS = 1024
NS_STEPS = 8
LANES = 128

outer_rate = 0.7
decay_rate = 0.9

HIGHEST = lax.Precision.HIGHEST


def mm(a, b):
    return lax.dot_general(
        a, b, (((1,), (0,)), ((), ())), precision=HIGHEST, preferred_element_type=jnp.float32
    )


def kernel(
    planes, peers, blocks,
    tensor_ref, delta_ref, moment_ref, params_ref,
    out_ref, new_moment_ref,
    delta, params, first_a, first_b, send_a, send_b, second_a, second_b, reduced, third,
    direction, matrix, sums, their_sums,
    load_sem, params_sem,
    s1a, r1a, s1b, r1b, s2a, r2a, s2b, r2b, s3, r3,
    gs, gr, gxs, gxr, gys, gyr, fas, far, fbs, fbr, ss, sr, up_sem, down_sem,
):
    rep = lax.axis_index("rep")
    shard = lax.axis_index("shard")
    x = rep % 2
    y = (rep // 2) % 2
    z = rep // 4
    nx, ny = 1 - x, 1 - y
    x_peer = {"rep": z * 4 + y * 2 + nx}
    y_peer = {"rep": z * 4 + ny * 2 + x}
    rows = delta.shape[3]
    half = rows // 2
    top, low = pl.ds(0, half), pl.ds(half, half)

    def plane(offset):
        return (z + offset) % planes

    def z_peer(offset):
        return {"rep": plane(offset) * 4 + y * 2 + x}

    order = [(k + 1) % planes for k in range(planes)]

    loads = []
    for k, offset in enumerate(order):
        at = plane(offset)
        copy = pltpu.make_async_copy(delta_ref.at[at], delta.at[at], load_sem.at[k])
        copy.start()
        loads.append(copy)
    params_copy = pltpu.make_async_copy(params_ref, params, params_sem)
    params_copy.start()

    barrier = pltpu.get_barrier_semaphore()
    targets = [x_peer, y_peer]
    targets += [{"shard": (shard + o) % peers} for o in range(1, peers)]
    for target in targets:
        pl.semaphore_signal(barrier, inc=1, device_id=target)

    def line(step):
        return {"rep": (z + step) * 4 + y * 2 + x}

    def tell(sem, distance):
        @pl.when((z >= 1) & (z + distance < planes))
        def _():
            pl.semaphore_signal(sem[0], inc=1, device_id=line(-1))

        @pl.when((z + 1 < planes) & (z - distance >= 0))
        def _():
            pl.semaphore_signal(sem[1], inc=1, device_id=line(1))

    def hear(distance):
        @pl.when(z + 1 + distance < planes)
        def _():
            pl.semaphore_wait(up_sem.at[distance], 1)

        @pl.when(z - 1 - distance >= 0)
        def _():
            pl.semaphore_wait(down_sem.at[distance], 1)

    def relay(distance):
        tell((up_sem.at[distance], down_sem.at[distance]), distance)

    tell((barrier, barrier), 0)
    inner = (z >= 1).astype(jnp.int32) + (z + 1 < planes).astype(jnp.int32)
    pl.semaphore_wait(barrier, len(targets) + inner)
    if planes > 2:
        relay(1)

    def remote(src, dst, send, recv, target):
        copy = pltpu.make_async_remote_copy(
            src_ref=src, dst_ref=dst, send_sem=send, recv_sem=recv, device_id=target
        )
        copy.start()
        return copy

    started = []

    def stage1(k):
        at = plane(order[k])
        loads[k].wait()
        a = remote(delta.at[at, :, nx, top], first_a.at[k], s1a.at[k], r1a.at[k], x_peer)
        b = remote(delta.at[at, ny, :, low], first_b.at[k], s1b.at[k], r1b.at[k], y_peer)
        started.extend([a, b])
        return a, b

    def stage2(k, first):
        at = plane(order[k])
        first[0].wait_recv()
        send_a[k] = delta[at, ny, x, top] + first_a[k, ny]
        a = remote(send_a.at[k], second_a.at[k], s2a.at[k], r2a.at[k], y_peer)
        first[1].wait_recv()
        send_b[k] = delta[at, y, nx, low] + first_b[k, nx]
        b = remote(send_b.at[k], second_b.at[k], s2b.at[k], r2b.at[k], x_peer)
        started.extend([a, b])
        return a, b

    def stage3(k, second):
        at = plane(order[k])
        second[0].wait_recv()
        reduced[k, top] = delta[at, y, x, top] + first_a[k, y] + second_a[k]
        second[1].wait_recv()
        reduced[k, low] = delta[at, y, x, low] + first_b[k, x] + second_b[k]
        if order[k] == 0:
            return None
        c = remote(reduced.at[k], third.at[k], s3.at[k], r3.at[k], z_peer(order[k]))
        started.append(c)
        return c

    ones = {}
    twos = {}
    threes = {}
    for k in range(min(3, planes)):
        ones[k] = stage1(k)

    lane = lax.broadcasted_iota(jnp.int32, (1, LANES), 1)
    member = [(lane == tensor_ref[b]).astype(jnp.float32) for b in range(blocks)]
    params_copy.wait()
    param_sums = jnp.zeros((1, LANES), jnp.float32)
    chunks = params.shape[0] // blocks
    for b in range(blocks):
        part = params[pl.ds(b, chunks, stride=blocks), :]
        param_sums += member[b] * jnp.sum(part * part)

    for k in range(planes):
        twos[k] = stage2(k, ones[k])
        if k + 3 < planes:
            ones[k + 3] = stage1(k + 3)
        if k == 0:
            for distance in range(1, planes - 2):
                hear(distance)
                relay(distance + 1)
        if k == 1 and planes > 2:
            hear(planes - 2)
        if k >= 1:
            threes[k - 1] = stage3(k - 1, twos[k - 1])
    threes[planes - 1] = stage3(planes - 1, twos[planes - 1])

    total = reduced[planes - 1]
    for k in range(planes - 1):
        threes[k].wait_recv()
        total = total + third[k]
    mean = total / (planes * 4)
    new_moment = decay_rate * moment_ref[...] + mean
    new_moment_ref[...] = new_moment
    direction[z, y, x] = mean + decay_rate * new_moment

    gathers = {}
    near = {}

    def spread(k):
        at = plane(-k)
        own = direction.at[at, y, x]
        a = remote(own, own, gxs.at[k], gxr.at[k], x_peer)
        b = remote(own, own, gys.at[k], gyr.at[k], y_peer)
        started.extend([a, b])
        near[k] = (a, b)

    forwards = []

    def forward(k):
        at = plane(-k)
        a, b = near[k]
        b.wait_recv()
        from_y = direction.at[at, ny, x, top]
        fa = remote(from_y, from_y, fas.at[k], far.at[k], x_peer)
        a.wait_recv()
        from_x = direction.at[at, y, nx, low]
        fb = remote(from_x, from_x, fbs.at[k], fbr.at[k], y_peer)
        started.extend([fa, fb])
        forwards.extend([fa, fb])

    own = direction.at[z, y, x]
    for k in range(1, planes):
        gathers[k] = remote(own, own, gs.at[k], gr.at[k], z_peer(k))
        started.append(gathers[k])
    spread(0)
    for k in range(1, planes):
        gathers[k].wait_recv()
        spread(k)
        forward(k - 1)
    forward(planes - 1)
    for copy in forwards:
        copy.wait_recv()

    flat = direction.reshape(planes * 4 * rows, LANES)
    cols = BLOCK_COLS // LANES
    eye = (
        lax.broadcasted_iota(jnp.int32, (BLOCK_ROWS, BLOCK_ROWS), 0)
        == lax.broadcasted_iota(jnp.int32, (BLOCK_ROWS, BLOCK_ROWS), 1)
    ).astype(jnp.float32)

    grams, firsts, polys, scales = [], [], [], []
    for b in range(blocks):
        for c in range(cols):
            matrix[b, :, pl.ds(c * LANES, LANES)] = flat[
                pl.ds(c * blocks + b, BLOCK_ROWS, stride=cols * blocks), :
            ]
        whole = matrix[b]
        gram = lax.dot_general(
            whole, whole, (((1,), (1,)), ((), ())),
            precision=HIGHEST, preferred_element_type=jnp.float32,
        )
        scale = 1.0 / jnp.sqrt(jnp.sum(gram * eye, keepdims=True) + 1.0)
        gram = gram * (scale * scale)
        scales.append(scale)
        grams.append(gram)
        firsts.append(gram)
        polys.append(None)
    for step in range(NS_STEPS):
        for b in range(blocks):
            gram = grams[b]
            factor = 1.5 * eye - 0.5 * gram
            polys[b] = factor if step == 0 else mm(polys[b], factor)
            if step < NS_STEPS - 1:
                grams[b] = mm(mm(gram, factor), factor)

    update_sums = jnp.zeros((1, LANES), jnp.float32)
    for b in range(blocks):
        norm = jnp.sum(mm(polys[b], firsts[b]) * polys[b])
        update_sums += member[b] * norm
    sums[0:1, :] = param_sums
    sums[1:2, :] = update_sums
    exchanges = []
    for o in range(1, peers):
        copy = remote(
            sums, their_sums.at[o - 1], ss.at[o - 1], sr.at[o - 1],
            {"shard": (shard + o) % peers},
        )
        exchanges.append(copy)
        started.append(copy)
    updates = [mm(polys[b] * scales[b], matrix[b]) for b in range(blocks)]
    for o, copy in enumerate(exchanges):
        copy.wait_recv()
        param_sums = param_sums + their_sums[o, 0:1, :]
        update_sums = update_sums + their_sums[o, 1:2, :]
    rate = outer_rate * jnp.sqrt(jnp.maximum(param_sums, 1.0) / jnp.maximum(update_sums, 1.0))
    for b in range(blocks):
        block_rate = jnp.sum(member[b] * rate, keepdims=True)
        for c in range(cols):
            at = pl.ds(c * blocks + b, BLOCK_ROWS, stride=cols * blocks)
            out_ref[at, :] = (
                params[at, :] - block_rate * updates[b][:, c * LANES : (c + 1) * LANES]
            )
    for copy in started:
        copy.wait_send()


def interleave(array):
    blocks, width = array.shape
    tiles = array.reshape(blocks, width // LANES, LANES)
    return tiles.transpose(1, 0, 2).reshape(blocks * width // LANES, LANES)


def deinterleave(array, blocks):
    tiles = array.reshape(array.shape[0] // blocks, blocks, LANES)
    return tiles.transpose(1, 0, 2).reshape(blocks, -1)


def shards(outer_params, replica_delta, momentum, tensor_of_block):
    blocks = outer_params.shape[0]
    replicas = lax.axis_size("rep")
    peers = lax.axis_size("shard")
    planes = replicas // 4
    moment = interleave(momentum)
    rows = moment.shape[0]
    half = rows // 2
    delta = interleave(replica_delta[0]).reshape(planes, 2, 2, rows, LANES)
    params = interleave(outer_params)
    f32 = jnp.float32
    vm = pltpu.VMEM
    dma = pltpu.SemaphoreType.DMA
    out, new_moment = pl.pallas_call(
        functools.partial(kernel, planes, peers, blocks),
        out_shape=(
            jax.ShapeDtypeStruct(params.shape, f32),
            jax.ShapeDtypeStruct(moment.shape, f32),
        ),
        in_specs=[
            pl.BlockSpec(memory_space=pltpu.SMEM),
            pl.BlockSpec(memory_space=pl.ANY),
            pl.BlockSpec(memory_space=pltpu.VMEM),
            pl.BlockSpec(memory_space=pl.ANY),
        ],
        out_specs=(
            pl.BlockSpec(memory_space=pltpu.VMEM),
            pl.BlockSpec(memory_space=pltpu.VMEM),
        ),
        scratch_shapes=[
            vm(delta.shape, f32),
            vm(params.shape, f32),
            vm((planes, 2, half, LANES), f32),
            vm((planes, 2, half, LANES), f32),
            vm((planes, half, LANES), f32),
            vm((planes, half, LANES), f32),
            vm((planes, half, LANES), f32),
            vm((planes, half, LANES), f32),
            vm((planes, rows, LANES), f32),
            vm((planes, rows, LANES), f32),
            vm(delta.shape, f32),
            vm((blocks, BLOCK_ROWS, BLOCK_COLS), f32),
            vm((2, LANES), f32),
            vm((peers, 2, LANES), f32),
            dma((planes,)),
            dma,
        ]
        + [dma((planes,))] * 20
        + [dma((peers,))] * 2
        + [pltpu.SemaphoreType.REGULAR((planes,))] * 2,
        compiler_params=pltpu.CompilerParams(collective_id=0, has_side_effects=True),
    )(tensor_of_block, delta, moment, params)
    return deinterleave(out, blocks), deinterleave(new_moment, blocks)


def solution(mesh):
    return jax.shard_map(
        shards,
        mesh=mesh,
        in_specs=(P("shard", None), P("rep", "shard", None), P("shard", "rep"), P("shard")),
        out_specs=(P("shard", None), P("shard", "rep")),
        check_vma=False,
    )
```

profile of v0, /device:TPU:0, one launch (start us, length us, event | category | flops | bytes accessed | tf_op | source)
XLA Modules:
  0.0 48.0 jit_solution(6038586842390981628)
XLA Ops:
  0.6 44.4 %shard_map.59 = (f32[2048,128]{1,0:T(8,128)}, f32[128,128]{1,0:T(8,128)}) custom-call(s32[2]{0:T(128)} %tensor_ref.1, f32[4,2,2,128,128]{4,3,2,1,0:T(8,128)} %bitcast.25, f32[128,128]{1,0:T(8,128)} %bitcast.28, f32[2048,128]{1,0:T(8,128)} %bitcast.26), custom_call_target="tpu_custom_call" | custom-call | tf_op jit(solution)/shard_map/pallas_call | solution.py:305
  45.0 0.0 copy-start
  45.0 2.3 %copy.13 = f32[2,131072]{1,0:T(2,128)} copy(f32[2,131072]{1,0:T(2,128)} %bitcast.27) | data formatting | bytes 2097152
  47.3 0.0 copy-done
  47.3 0.6 %copy.14 = f32[2,8192]{1,0:T(2,128)} copy(f32[2,8192]{1,0:T(2,128)S(1)} %bitcast.29) | data formatting | bytes 131072
Async XLA Ops:
  45.0 2.3 %copy-start = (f32[128,128]{1,0:T(8,128)S(1)}, f32[128,128]{1,0:T(8,128)}, u32[]{:S(2)}) copy-start(f32[128,128]{1,0:T(8,128)} %get-tuple-element.5) | copy-start | bytes 196612
where the time goes:
time: 48.6 us; the launch traced here: 48 us
  Pallas kernels  44.4 us (91%)
  local copies, waits for them, and re-layouts  2.93 us (6%)
  between operations  0.65 us (1%)
    pallas_call x1, Pallas kernels, shards(): pl.pallas_call(functools.partial(kernel, planes, peers, blocks), out_shap...  44.4 us
    unnamed x4, local copies, waits for them, and re-layouts  2.93 us

commit v1 on v0

--- a/solution.py
+++ b/solution.py
@@ -11,26 +11,39 @@
 BLOCK_COLS = 1024
 NS_STEPS = 8
 LANES = 128
+VMEM_BYTES = 16 * 1024 * 1024
 
 outer_rate = 0.7
 decay_rate = 0.9
 
-HIGHEST = lax.Precision.HIGHEST
+
+def split(a):
+    high = a.astype(jnp.bfloat16)
+    return high, (a - high.astype(jnp.float32)).astype(jnp.bfloat16)
+
+
+def left(a):
+    return jnp.concatenate(split(a), axis=1)
+
+
+def right(b):
+    pair = jnp.concatenate(split(b), axis=1)
+    return jnp.concatenate([pair, pair], axis=0)
 
 
 def mm(a, b):
-    return lax.dot_general(
-        a, b, (((1,), (0,)), ((), ())), precision=HIGHEST, preferred_element_type=jnp.float32
-    )
+    both = jnp.dot(a, b, preferred_element_type=jnp.float32)
+    half = both.shape[1] // 2
+    return both[:, :half] + both[:, half:]
 
 
 def kernel(
     planes, peers, blocks,
     tensor_ref, delta_ref, moment_ref, params_ref,
-    out_ref, new_moment_ref,
-    delta, params, first_a, first_b, send_a, send_b, second_a, second_b, reduced, third,
+    update_ref, params, rate_ref, new_moment_ref,
+    delta, moment, first_a, first_b, send_a, send_b, second_a, second_b, reduced, third,
     direction, matrix, sums, their_sums,
-    load_sem, params_sem,
+    load_sem, params_sem, moment_sem,
     s1a, r1a, s1b, r1b, s2a, r2a, s2b, r2b, s3, r3,
     gs, gr, gxs, gxr, gys, gyr, fas, far, fbs, fbr, ss, sr, up_sem, down_sem,
 ):
@@ -60,8 +73,17 @@
         copy = pltpu.make_async_copy(delta_ref.at[at], delta.at[at], load_sem.at[k])
         copy.start()
         loads.append(copy)
-    params_copy = pltpu.make_async_copy(params_ref, params, params_sem)
-    params_copy.start()
+    moment_copy = pltpu.make_async_copy(moment_ref, moment, moment_sem)
+    moment_copy.start()
+    cols = BLOCK_COLS // LANES
+    params_copies = []
+    for b in range(blocks):
+        for c in range(cols):
+            copy = pltpu.make_async_copy(
+                params_ref.at[:, c, b], params.at[b, c], params_sem.at[b * cols + c]
+            )
+            copy.start()
+            params_copies.append(copy)
 
     barrier = pltpu.get_barrier_semaphore()
     targets = [x_peer, y_peer]
@@ -147,11 +169,11 @@
 
     lane = lax.broadcasted_iota(jnp.int32, (1, LANES), 1)
     member = [(lane == tensor_ref[b]).astype(jnp.float32) for b in range(blocks)]
-    params_copy.wait()
+    for copy in params_copies:
+        copy.wait()
     param_sums = jnp.zeros((1, LANES), jnp.float32)
-    chunks = params.shape[0] // blocks
-    for b in range(blocks):
-        part = params[pl.ds(b, chunks, stride=blocks), :]
+    for b in range(blocks):
+        part = params[b]
         param_sums += member[b] * jnp.sum(part * part)
 
     for k in range(planes):
@@ -173,7 +195,8 @@
         threes[k].wait_recv()
         total = total + third[k]
     mean = total / (planes * 4)
-    new_moment = decay_rate * moment_ref[...] + mean
+    moment_copy.wait()
+    new_moment = decay_rate * moment[...] + mean
     new_moment_ref[...] = new_moment
     direction[z, y, x] = mean + decay_rate * new_moment
 
@@ -216,23 +239,25 @@
         copy.wait_recv()
 
     flat = direction.reshape(planes * 4 * rows, LANES)
-    cols = BLOCK_COLS // LANES
     eye = (
         lax.broadcasted_iota(jnp.int32, (BLOCK_ROWS, BLOCK_ROWS), 0)
         == lax.broadcasted_iota(jnp.int32, (BLOCK_ROWS, BLOCK_ROWS), 1)
     ).astype(jnp.float32)
+    top_rows, low_rows = pl.ds(0, BLOCK_ROWS), pl.ds(BLOCK_ROWS, BLOCK_ROWS)
 
     grams, firsts, polys, scales = [], [], [], []
     for b in range(blocks):
         for c in range(cols):
-            matrix[b, :, pl.ds(c * LANES, LANES)] = flat[
-                pl.ds(c * blocks + b, BLOCK_ROWS, stride=cols * blocks), :
-            ]
+            high, low_part = split(flat[pl.ds(c * blocks + b, BLOCK_ROWS, stride=cols * blocks), :])
+            matrix[b, top_rows, pl.ds(c * LANES, LANES)] = high
+            matrix[b, low_rows, pl.ds(c * LANES, LANES)] = low_part
+    for b in range(blocks):
         whole = matrix[b]
-        gram = lax.dot_general(
-            whole, whole, (((1,), (1,)), ((), ())),
-            precision=HIGHEST, preferred_element_type=jnp.float32,
+        quads = lax.dot_general(
+            whole, whole, (((1,), (1,)), ((), ())), preferred_element_type=jnp.float32
         )
+        halves = quads[:BLOCK_ROWS] + quads[BLOCK_ROWS:]
+        gram = halves[:, :BLOCK_ROWS] + halves[:, BLOCK_ROWS:]
         scale = 1.0 / jnp.sqrt(jnp.sum(gram * eye, keepdims=True) + 1.0)
         gram = gram * (scale * scale)
         scales.append(scale)
@@ -240,17 +265,25 @@
         firsts.append(gram)
         polys.append(None)
     for step in range(NS_STEPS):
+        last = step == NS_STEPS - 1
+        factors = [1.5 * eye - 0.5 * grams[b] for b in range(blocks)]
+        rights = [right(factors[b]) for b in range(blocks)]
+        halfway = [None] * blocks
         for b in range(blocks):
-            gram = grams[b]
-            factor = 1.5 * eye - 0.5 * gram
-            polys[b] = factor if step == 0 else mm(polys[b], factor)
-            if step < NS_STEPS - 1:
-                grams[b] = mm(mm(gram, factor), factor)
+            if not last:
+                halfway[b] = mm(left(grams[b]), rights[b])
+        for b in range(blocks):
+            polys[b] = factors[b] if step == 0 else mm(left(polys[b]), rights[b])
+        for b in range(blocks):
+            if not last:
+                grams[b] = mm(left(halfway[b]), rights[b])
 
     update_sums = jnp.zeros((1, LANES), jnp.float32)
-    for b in range(blocks):
-        norm = jnp.sum(mm(polys[b], firsts[b]) * polys[b])
+    scaled = []
+    for b in range(blocks):
+        norm = jnp.sum(mm(left(polys[b]), right(firsts[b])) * polys[b])
         update_sums += member[b] * norm
+        scaled.append(left(polys[b] * scales[b]))
     sums[0:1, :] = param_sums
     sums[1:2, :] = update_sums
     exchanges = []
@@ -261,7 +294,19 @@
         )
         exchanges.append(copy)
         started.append(copy)
-    updates = [mm(polys[b] * scales[b], matrix[b]) for b in range(blocks)]
+    for b in range(blocks):
+        for c in range(0, cols, 2):
+            high = matrix[b, top_rows, pl.ds(c * LANES, 2 * LANES)]
+            low_part = matrix[b, low_rows, pl.ds(c * LANES, 2 * LANES)]
+            update = jnp.dot(
+                scaled[b], jnp.concatenate([high, high], axis=0),
+                preferred_element_type=jnp.float32,
+            ) + jnp.dot(
+                scaled[b], jnp.concatenate([low_part, low_part], axis=0),
+                preferred_element_type=jnp.float32,
+            )
+            update_ref[b, c] = update[:, :LANES]
+            update_ref[b, c + 1] = update[:, LANES:]
     for o, copy in enumerate(exchanges):
         copy.wait_recv()
         param_sums = param_sums + their_sums[o, 0:1, :]
@@ -269,13 +314,28 @@
     rate = outer_rate * jnp.sqrt(jnp.maximum(param_sums, 1.0) / jnp.maximum(update_sums, 1.0))
     for b in range(blocks):
         block_rate = jnp.sum(member[b] * rate, keepdims=True)
-        for c in range(cols):
-            at = pl.ds(c * blocks + b, BLOCK_ROWS, stride=cols * blocks)
-            out_ref[at, :] = (
-                params[at, :] - block_rate * updates[b][:, c * LANES : (c + 1) * LANES]
-            )
+        rate_ref[b] = jnp.broadcast_to(block_rate, rate_ref.shape[1:])
     for copy in started:
         copy.wait_send()
+
+
+def apply(update_ref, params_ref, rate_ref, moment_ref, out_ref, new_moment_ref, staged, sems, moment_sem):
+    blocks, cols = update_ref.shape[:2]
+    moment_copy = pltpu.make_async_copy(moment_ref, new_moment_ref, moment_sem)
+    moment_copy.start()
+    copies = []
+    for b in range(blocks):
+        rate = rate_ref[b, 0:1, :]
+        for c in range(cols):
+            staged[b, c] = params_ref[b, c] - rate * update_ref[b, c]
+            copy = pltpu.make_async_copy(
+                staged.at[b, c], out_ref.at[:, c, b], sems.at[b * cols + c]
+            )
+            copy.start()
+            copies.append(copy)
+    for copy in copies:
+        copy.wait()
+    moment_copy.wait()
 
 
 def interleave(array):
@@ -291,6 +351,7 @@
 
 def shards(outer_params, replica_delta, momentum, tensor_of_block):
     blocks = outer_params.shape[0]
+    cols = BLOCK_COLS // LANES
     replicas = lax.axis_size("rep")
     peers = lax.axis_size("shard")
     planes = replicas // 4
@@ -298,29 +359,26 @@
     rows = moment.shape[0]
     half = rows // 2
     delta = interleave(replica_delta[0]).reshape(planes, 2, 2, rows, LANES)
-    params = interleave(outer_params)
+    params = interleave(outer_params).reshape(BLOCK_ROWS, cols, blocks, LANES)
     f32 = jnp.float32
     vm = pltpu.VMEM
     dma = pltpu.SemaphoreType.DMA
-    out, new_moment = pl.pallas_call(
+    tiles = (blocks, cols, BLOCK_ROWS, LANES)
+    vmem = pl.BlockSpec(memory_space=pltpu.VMEM)
+    hbm = pl.BlockSpec(memory_space=pltpu.HBM)
+    update, held, rate, moved = pl.pallas_call(
         functools.partial(kernel, planes, peers, blocks),
         out_shape=(
-            jax.ShapeDtypeStruct(params.shape, f32),
-            jax.ShapeDtypeStruct(moment.shape, f32),
+            vm(tiles, f32),
+            vm(tiles, f32),
+            vm((blocks, 8, LANES), f32),
+            vm(moment.shape, f32),
         ),
-        in_specs=[
-            pl.BlockSpec(memory_space=pltpu.SMEM),
-            pl.BlockSpec(memory_space=pl.ANY),
-            pl.BlockSpec(memory_space=pltpu.VMEM),
-            pl.BlockSpec(memory_space=pl.ANY),
-        ],
-        out_specs=(
-            pl.BlockSpec(memory_space=pltpu.VMEM),
-            pl.BlockSpec(memory_space=pltpu.VMEM),
-        ),
+        in_specs=[pl.BlockSpec(memory_space=pltpu.SMEM), hbm, hbm, hbm],
+        out_specs=(vmem, vmem, vmem, vmem),
         scratch_shapes=[
             vm(delta.shape, f32),
-            vm(params.shape, f32),
+            vm(moment.shape, f32),
             vm((planes, 2, half, LANES), f32),
             vm((planes, 2, half, LANES), f32),
             vm((planes, half, LANES), f32),
@@ -330,17 +388,32 @@
             vm((planes, rows, LANES), f32),
             vm((planes, rows, LANES), f32),
             vm(delta.shape, f32),
-            vm((blocks, BLOCK_ROWS, BLOCK_COLS), f32),
+            vm((blocks, 2 * BLOCK_ROWS, BLOCK_COLS), jnp.bfloat16),
             vm((2, LANES), f32),
             vm((peers, 2, LANES), f32),
             dma((planes,)),
+            dma((blocks * cols,)),
             dma,
         ]
         + [dma((planes,))] * 20
         + [dma((peers,))] * 2
         + [pltpu.SemaphoreType.REGULAR((planes,))] * 2,
-        compiler_params=pltpu.CompilerParams(collective_id=0, has_side_effects=True),
-    )(tensor_of_block, delta, moment, params)
+        compiler_params=pltpu.CompilerParams(
+            collective_id=0, has_side_effects=True, vmem_limit_bytes=VMEM_BYTES
+        ),
+    )(*(pltpu.with_memory_space_constraint(a, pltpu.HBM) for a in (tensor_of_block, delta, moment, params)))
+    out, new_moment = pl.pallas_call(
+        apply,
+        out_shape=(
+            jax.ShapeDtypeStruct(params.shape, f32),
+            jax.ShapeDtypeStruct(moment.shape, f32),
+        ),
+        in_specs=[vmem] * 4,
+        out_specs=(hbm, hbm),
+        scratch_shapes=[vm(tiles, f32), dma((blocks * cols,)), dma],
+        compiler_params=pltpu.CompilerParams(vmem_limit_bytes=8 * 1024 * 1024),
+    )(update, held, rate, moved)
+    out = out.reshape(-1, LANES)
     return deinterleave(out, blocks), deinterleave(new_moment, blocks)
 
 

time: 48.6 us -> 42.1 us (0.87)
  Pallas kernels: 44.4 us -> 41.3 us
  local copies, waits for them, and re-layouts: 2.93 us -> 0 us
    pallas_call x1, Pallas kernels: 44.4 us -> 40.1 us  [shards(): pl.pallas_call(functools.partial(kernel, planes, peers, blocks), out_shap...]
    unnamed x4 -> x0, local copies, waits for them, and re-layouts: 2.93 us -> none
    pallas_call x0 -> x1, Pallas kernels: none -> 1.13 us  [shards(): pl.pallas_call(apply, out_shape=(jax.ShapeDtypeStruct(params.shape, f32),...]
where the time goes in v1:
time: 42.1 us; the launch traced here: 41.9 us
  Pallas kernels  41.3 us (98%)
  between operations  0.64 us (2%)
    pallas_call x1, Pallas kernels, shards(): pl.pallas_call(functools.partial(kernel, planes, peers, blocks), out_shap...  40.1 us
    pallas_call x1, Pallas kernels, shards(): pl.pallas_call(apply, out_shape=(jax.ShapeDtypeStruct(params.shape, f32),...  1.13 us

profile of v1, /device:TPU:0, one launch (start us, length us, event | category | flops | bytes accessed | tf_op | source)
XLA Modules:
  0.0 41.9 jit_solution(5914263660429692130)
XLA Ops:
  0.6 40.1 %shard_map.59 = (f32[2,8,128,128]{3,2,1,0:T(8,128)S(1)}, f32[2,8,128,128]{3,2,1,0:T(8,128)S(1)}, f32[2,8,128]{2,1,0:T(8,128)S(1)}, f32[128,128]{1,0:T(8,128)S(1)}) custom-call(s32[2]{0:T(128)} %tensor_ref.1, f32[4,2,2,128,128]{4,3,2,1,0:T(8,128)} %bitcast.25, f32[128,128]{1,0:T(8,128)} %bitcast.27, f32[128,8,2,128]{3,2,1,0:T(2,128)} %bitcast.26), custom_call_target="tpu_custom_call" | custom-call | tf_op jit(solution)/shard_map/pallas_call | solution.py:369
  40.8 1.1 %shard_map.60 = (f32[128,8,2,128]{3,2,1,0:T(2,128)}, f32[128,128]{1,0:T(8,128)}) custom-call(f32[2,8,128,128]{3,2,1,0:T(8,128)S(1)} %get-tuple-element.8.update_ref, f32[2,8,128,128]{3,2,1,0:T(8,128)S(1)} %get-tuple-element.9.params_ref, f32[2,8,128]{2,1,0:T(8,128)S(1)} %get-tuple-element.10.rate_ref, f32[128,128]{1,0:T(8,128)S(1)} %get-tuple-element.11.moment_ref), custom_call_target="tpu_custom_call" | custom-call | tf_op jit(solution)/shard_map/pallas_call | solution.py:405
